TPU v7x, 32 devices: a whole 2x2x4 slice. The times are simulated.
32 devices in a mesh: seq: 8 (over z, y), batch: 4 (over x, core).
Axes of the slice: x: 2, y: 2, z: 4, core: 2. Of those that a mesh axis runs over, the one named last changes fastest.
Arguments:
- tokens: bfloat16 [4, 8192, 1024], P('batch', 'seq'), may hold values from -6 to 6
- logits: bfloat16 [4, 8192, 256], P('batch', 'seq'), may hold values from -160 to 160
- slot_grad: bfloat16 [4, 256, 1024], P('batch', 'seq'), may hold values from -6 to 6
- phi_param: bfloat16 [1024, 256], P('seq'), may hold values from -0.1875 to 0.1875
Outputs:
- token_grad: bfloat16 [4, 8192, 1024], P('batch', 'seq')
- phi_grad: float32 [1024, 256], P('seq')
All inputs are finite; a program needn't handle non-finite values.
Results may differ from a plain program's by a relative error of at most 0.0049.
Values may be sent and summed in bfloat16 or wider, within the bound.
A program may use at most 64 MiB of HBM per device.

v0:
```python
import jax
import jax.numpy as jnp
from jax import lax
from jax.sharding import PartitionSpec as P


def per_device(tokens, logits, slot_grad, phi_param):
    inputs = tokens[0]
    scores = logits[0].astype(jnp.float32)
    upstream, phi_full = (
        lax.all_gather(slot_grad[0], "seq", axis=0, tiled=True),
        lax.all_gather(phi_param, "seq", axis=0, tiled=True),
    )
    weight_grad = lax.dot_general(
        inputs, upstream, (((1,), (1,)), ((), ())), preferred_element_type=jnp.float32
    )
    col_peak = lax.pmax(jnp.max(scores, axis=0, keepdims=True), "seq")
    raw_weights = jnp.exp(scores - col_peak)
    col_total = lax.psum(jnp.sum(raw_weights, axis=0, keepdims=True), "seq")
    dispatch = raw_weights / col_total
    col_dot = lax.psum(jnp.sum(dispatch * weight_grad, axis=0, keepdims=True), "seq")
    logit_grad = (dispatch * (weight_grad - col_dot)).astype(jnp.bfloat16)
    dispatch_low = dispatch.astype(jnp.bfloat16)
    grad_scale = float(lax.axis_size("seq") * inputs.shape[0] // 16)
    token_sum = jnp.dot(dispatch_low, upstream, preferred_element_type=jnp.float32)
    token_sum = token_sum + lax.dot_general(
        logit_grad, phi_full, (((1,), (1,)), ((), ())), preferred_element_type=jnp.float32
    )
    token_grad = (grad_scale * token_sum).astype(jnp.bfloat16)[None]
    phi_terms = lax.dot_general(
        inputs, logit_grad, (((0,), (0,)), ((), ())), preferred_element_type=jnp.float32
    )
    phi_share = lax.psum_scatter(phi_terms, "seq", scatter_dimension=0, tiled=True)
    phi_grad = lax.psum(phi_share, "batch")
    return (token_grad, phi_grad)


def solution(mesh):
    return jax.shard_map(
        per_device,
        mesh=mesh,
        in_specs=(
            P("batch", "seq", None),
            P("batch", "seq", None),
            P("batch", "seq", None),
            P("seq", None),
        ),
        out_specs=(P("batch", "seq", None), P("seq", None)),
        check_vma=False,
    )
```

profile of v0, /device:TPU:0, one launch (start us, length us, event | category | flops | bytes accessed | tf_op | source)
XLA Modules:
  0.0 210.9 jit_solution(2274995212261977552)
XLA Ops:
  7.2 0.0 copy-start
  7.2 0.0 reduce-scatter.2.cloned.1.call-start
  7.2 1.3 reduce_max.16
  8.6 23.2 %pmax.7 = f32[256]{0:T(256)S(1)} all-reduce(bf16[256]{0:T(256)(128)(2,1)S(1)} %reduce_max.16), channel_id=1, replica_groups=mesh['seq'=8,'batch'=4] {'seq'}, use_global_device_ids=true, to_apply=%region_1.0 | all-reduce | flops 256 | bytes 1536 | tf_op jit(solution)/shard_map/pmax | solution.py:17
  31.7 1.3 fusion.10
  33.0 17.1 %psum.21 = f32[256]{0:T(256)S(1)} all-reduce(f32[256]{0:T(256)S(1)} %fusion.10), channel_id=1, replica_groups=mesh['seq'=8,'batch'=4] {'seq'}, use_global_device_ids=true, to_apply=%region_3.0 | all-reduce | flops 256 | bytes 2048 | tf_op jit(solution)/shard_map/psum | solution.py:19
  50.1 31.5 %all-gather = bf16[1,256,1024]{2,1,0:T(8,128)(2,1)S(1)} all-gather(bf16[1,32,1024]{2,1,0:T(8,128)(2,1)} %param.6), channel_id=2, replica_groups=mesh['seq'=8,'batch'=4] {'seq'}, dimensions={1}, use_global_device_ids=true | all-gather | bytes 589824 | tf_op jit(solution)/shard_map/all_gather | solution.py:11
  81.6 0.0 copy-done
  81.6 0.0 copy-start.2
  81.6 3.0 %multiply_reduce_fusion = (f32[256]{0:T(256)S(1)}, f32[1024,256]{1,0:T(8,128)}) fusion(f32[256]{0:T(256)S(1)} %psum.21, f32[256]{0:T(256)S(1)} %pmax.7, bf16[1,1024,256]{2,1,0:T(8,128)(2,1)} %param.5, bf16[1,256,1024]{2,1,0:T(8,128)(2,1)S(1)} %all-gather, bf16[1,1024,1024]{2,1,0:T(8,128)(2,1)S(1)} %copy-done), kind=kOutput, calls=%fused_computation.12 | convolution fusion | flops 538181376 | bytes 4197376 | tf_op jit(solution)/shard_map/dot_general | solution.py:14
  84.6 0.0 copy-done.2
  84.6 19.4 %psum.22 = f32[256]{0:T(256)S(1)} all-reduce(f32[256]{0:T(256)S(1)} %get-tuple-element.4), channel_id=1, replica_groups=mesh['seq'=8,'batch'=4] {'seq'}, use_global_device_ids=true, to_apply=%region_5.0 | all-reduce | flops 256 | bytes 2048 | tf_op jit(solution)/shard_map/psum | solution.py:21
  103.9 0.0 copy-done.1
  103.9 3.0 %fusion.5 = f32[1024,256]{0,1:T(8,128)} fusion(bf16[1,1024,1024]{2,1,0:T(8,128)(2,1)S(1)} %copy-done, f32[1024,256]{1,0:T(8,128)} %get-tuple-element.5, f32[256]{0:T(256)S(1)} %psum.22, f32[256]{0:T(256)S(1)} %psum.21, f32[256]{0:T(256)S(1)} %pmax.7, bf16[1,1024,256]{2,1,0:T(8,128)(2,1)S(1)} %copy-done.1), kind=kOutput, calls=%fused_computation.6 | convolution fusion | flops 538443776 | bytes 4721664 | tf_op jit(solution)/shard_map/dot_general | solution.py:30
  107.0 0.0 reduce-scatter.2.cloned.1.call-update
  107.0 0.0 all-reduce.2.cloned.1.call-start
  107.0 0.0 copy-done.3
  107.0 31.8 %all_gather.7 = bf16[1024,256]{1,0:T(8,128)(2,1)S(1)} all-gather(bf16[128,256]{1,0:T(8,128)(2,1)S(1)} %copy-done.3), channel_id=1, replica_groups=mesh['seq'=8,'batch'=4] {'seq'}, dimensions={0}, use_global_device_ids=true | all-gather | bytes 589824 | tf_op jit(solution)/shard_map/all_gather | solution.py:12
  138.8 3.7 %fusion.12 = f32[1024,1024]{1,0:T(8,128)} fusion(bf16[1,256,1024]{2,1,0:T(8,128)(2,1)} %copy-done.2, bf16[1,1024,256]{2,1,0:T(8,128)(2,1)S(1)} %copy-done.1, f32[256]{0:T(256)S(1)} %psum.21, f32[256]{0:T(256)S(1)} %pmax.7), kind=kOutput, calls=%fused_computation.14 | convolution fusion | flops 537919488 | bytes 5244928 | tf_op jit(solution)/shard_map/dot_general | solution.py:25
  142.5 26.9 %reduce-scatter.2.cloned.1.call-done = f32[128,256]{0,1:T(8,128)} async-done(((f32[1024,256]{0,1:T(8,128)}), f32[128,256]{0,1:T(8,128)}) %reduce-scatter.2.cloned.1.call-update) | async-done | bytes 131088 | tf_op jit(solution)/shard_map/reduce_scatter | solution.py:33
  169.4 0.0 all-reduce.2.cloned.1.call-update
  169.4 4.7 %fusion.4 = bf16[1,1024,1024]{2,1,0:T(8,128)(2,1)} fusion(f32[1024,1024]{1,0:T(8,128)} %fusion.12, bf16[1024,256]{1,0:T(8,128)(2,1)S(1)} %all_gather.7, f32[1024,256]{1,0:T(8,128)} %get-tuple-element.5, f32[256]{0:T(256)S(1)} %psum.22, f32[256]{0:T(256)S(1)} %psum.21, f32[256]{0:T(256)S(1)} %pmax.7, bf16[1,1024,256]{2,1,0:T(8,128)(2,1)S(1)} %copy-done.1), kind=kOutput, calls=%fused_computation.5 | convolution fusion | flops 541589504 | bytes 8391680 | tf_op jit(solution)/shard_map/dot_general | solution.py:26
  174.1 28.3 %all-reduce.2.cloned.1.call-done = f32[128,256]{0,1:T(8,128)} async-done(((f32[128,256]{0,1:T(8,128)}), f32[128,256]{0,1:T(8,128)}) %all-reduce.2.cloned.1.call-update) | async-done | bytes 131088 | tf_op jit(solution)/shard_map/psum | solution.py:34
  202.4 1.7 copy.6
  (2 shorter events, 0.0 us)
Async XLA Ops:
  7.2 74.4 %copy-start = (bf16[1,1024,1024]{2,1,0:T(8,128)(2,1)S(1)}, bf16[1,1024,1024]{2,1,0:T(8,128)(2,1)}, u32[]{:S(2)}) copy-start(bf16[1,1024,1024]{2,1,0:T(8,128)(2,1)} %param.4) | copy-start | bytes 6291460
  7.2 162.2 %reduce-scatter.2.cloned.1.call-start = ((), (), s32[]{:S(2)}) async-start(), calls=%async_computation.1 | async-start | bytes 1179648 | tf_op jit(solution)/shard_map/reduce_scatter | solution.py:33
  81.6 3.0 %copy-start.2 = (bf16[1,256,1024]{2,1,0:T(8,128)(2,1)}, bf16[1,256,1024]{2,1,0:T(8,128)(2,1)S(1)}, u32[]{:S(2)}) copy-start(bf16[1,256,1024]{2,1,0:T(8,128)(2,1)S(1)} %all-gather) | copy-start | bytes 1572868
  81.6 22.3 %copy-start.1 = (bf16[1,1024,256]{2,1,0:T(8,128)(2,1)S(1)}, bf16[1,1024,256]{2,1,0:T(8,128)(2,1)}, u32[]{:S(2)}) copy-start(bf16[1,1024,256]{2,1,0:T(8,128)(2,1)} %param.5) | copy-start | bytes 1572868
  103.9 3.1 %copy-start.3 = (bf16[128,256]{1,0:T(8,128)(2,1)S(1)}, bf16[128,256]{1,0:T(8,128)(2,1)}, u32[]{:S(2)}) copy-start(bf16[128,256]{1,0:T(8,128)(2,1)} %param.7) | copy-start | bytes 196612
  107.0 95.4 %all-reduce.2.cloned.1.call-start = ((), (), s32[]{:S(2)}) async-start(), calls=%async_computation.2 | async-start | bytes 262144 | tf_op jit(solution)/shard_map/psum | solution.py:34
Sparse Core Ops, SparseCore 0:
  107.1 62.2 reduce-scatter.1
  171.7 30.6 all-reduce.1
where the time goes:
time: 211 us
  blocking collectives  123 us (58%)
  waiting for transfers between devices  55.3 us (26%)
  matrix products  14.4 us (7%)
  between operations  14.1 us (7%)
  other arithmetic  2.61 us (1%)
    all_gather x1, blocking collectives, per_device(): lax.all_gather(phi_param, 'seq', axis=0, tiled=True)  31.8 us
    all_gather x1, blocking collectives, per_device(): lax.all_gather(slot_grad[0], 'seq', axis=0, tiled=True)  31.5 us
    psum x1, waiting for transfers between devices, per_device(): phi_grad = lax.psum(phi_share, 'batch')  28.3 us
    reduce_scatter x1, waiting for transfers between devices, per_device(): lax.psum_scatter(phi_terms, 'seq', scatter_dimension=0, tiled=True)  26.9 us
    pmax x1, blocking collectives, per_device(): col_peak = lax.pmax(jnp.max(scores, axis=0, keepdims=True), 'seq')  23.2 us
    psum x1, blocking collectives, per_device(): lax.psum(jnp.sum(dispatch * weight_grad, axis=0, keepdims=True), 'seq')  19.4 us
    psum x1, blocking collectives, per_device(): col_total = lax.psum(jnp.sum(raw_weights, axis=0, keepdims=True), 'seq')  17.1 us
    dot_general x1, matrix products, per_device(): lax.dot_general(logit_grad, phi_full, (((1,), (1,)), ((), ())), preferred...  4.68 us
  transfers between devices with their start and end apart: 2, of which 2 were waited for; matrix products, arithmetic and copies ran while one was open for 4% of the time, Pallas kernels for 0%

commit v1 on v0

--- a/solution.py
+++ b/solution.py
@@ -31,7 +31,7 @@
         inputs, logit_grad, (((0,), (0,)), ((), ())), preferred_element_type=jnp.float32
     )
     phi_share = lax.psum_scatter(phi_terms, "seq", scatter_dimension=0, tiled=True)
-    phi_grad = lax.psum(phi_share, "batch")
+    phi_grad = jnp.sum(lax.all_gather(phi_share, "batch"), axis=0)
     return (token_grad, phi_grad)
 
 

time: 211 us -> 185 us (0.88)
  waiting for transfers between devices: 55.3 us -> 27.1 us
  blocking collectives: 123 us -> 130 us
  matrix products: 14.4 us -> 8.78 us
    psum x1 -> x0, waiting for transfers between devices: 28.3 us -> none  [per_device(): phi_grad = lax.psum(phi_share, 'batch')]
    all_gather x0 -> x1, blocking collectives: none -> 7.36 us  [per_device(): phi_grad = jnp.sum(lax.all_gather(phi_share, 'batch'), axis=0)]
    dot_general x1, matrix products: 3.68 us -> 0.71 us  [per_device(): jnp.dot(dispatch_low, upstream, preferred_element_type=jnp.float32)]
    dot_general x1, matrix products: 4.68 us -> 2.19 us  [per_device(): lax.dot_general(logit_grad, phi_full, (((1,), (1,)), ((), ())), preferred...]
  transfers between devices with their start and end apart: 2 -> 1, of which waited for: 2 -> 1; matrix products, arithmetic and copies ran while one was open for 4% -> 2% of each run, Pallas kernels for 0% -> 0%
where the time goes in v1:
time: 185 us
  blocking collectives  130 us (70%)
  waiting for transfers between devices  27.1 us (15%)
  between operations  14.1 us (8%)
  matrix products  8.78 us (5%)
  other arithmetic  2.91 us (2%)
    all_gather x1, blocking collectives, per_device(): lax.all_gather(phi_param, 'seq', axis=0, tiled=True)  31.8 us
    all_gather x1, blocking collectives, per_device(): lax.all_gather(slot_grad[0], 'seq', axis=0, tiled=True)  31.4 us
    reduce_scatter x1, waiting for transfers between devices, per_device(): lax.psum_scatter(phi_terms, 'seq', scatter_dimension=0, tiled=True)  27.1 us
    pmax x1, blocking collectives, per_device(): col_peak = lax.pmax(jnp.max(scores, axis=0, keepdims=True), 'seq')  23.2 us
    psum x1, blocking collectives, per_device(): lax.psum(jnp.sum(dispatch * weight_grad, axis=0, keepdims=True), 'seq')  19.4 us
    psum x1, blocking collectives, per_device(): col_total = lax.psum(jnp.sum(raw_weights, axis=0, keepdims=True), 'seq')  17.1 us
    all_gather x1, blocking collectives, per_device(): phi_grad = jnp.sum(lax.all_gather(phi_share, 'batch'), axis=0)  7.36 us
  transfers between devices with their start and end apart: 1, of which 1 were waited for; matrix products, arithmetic and copies ran while one was open for 2% of the time, Pallas kernels for 0%

profile of v1, /device:TPU:0, one launch (start us, length us, event | category | flops | bytes accessed | tf_op | source)
XLA Modules:
  0.0 184.6 jit_solution(1900664875650321618)
XLA Ops:
  7.2 0.0 copy-start
  7.2 0.0 reduce-scatter.2.cloned.1.call-start
  7.2 1.3 reduce_max.16
  8.6 23.2 %pmax.7 = f32[256]{0:T(256)S(1)} all-reduce(bf16[256]{0:T(256)(128)(2,1)S(1)} %reduce_max.16), channel_id=1, replica_groups=mesh['seq'=8,'batch'=4] {'seq'}, use_global_device_ids=true, to_apply=%region_1.0 | all-reduce | flops 256 | bytes 1536 | tf_op jit(solution)/shard_map/pmax | solution.py:17
  31.7 1.3 fusion.10
  33.0 17.1 %psum.14 = f32[256]{0:T(256)S(1)} all-reduce(f32[256]{0:T(256)S(1)} %fusion.10), channel_id=1, replica_groups=mesh['seq'=8,'batch'=4] {'seq'}, use_global_device_ids=true, to_apply=%region_3.0 | all-reduce | flops 256 | bytes 2048 | tf_op jit(solution)/shard_map/psum | solution.py:19
  50.1 31.4 %all-gather = bf16[1,256,1024]{2,1,0:T(8,128)(2,1)S(1)} all-gather(bf16[1,32,1024]{2,1,0:T(8,128)(2,1)} %param.6), channel_id=2, replica_groups=mesh['seq'=8,'batch'=4] {'seq'}, dimensions={1}, use_global_device_ids=true | all-gather | bytes 589824 | tf_op jit(solution)/shard_map/all_gather | solution.py:11
  81.5 0.0 copy-done
  81.5 0.0 copy-start.1
  81.5 2.8 %multiply_reduce_fusion = (f32[256]{0:T(256)S(1)}, f32[1024,256]{1,0:T(8,128)}) fusion(f32[256]{0:T(256)S(1)} %psum.14, f32[256]{0:T(256)S(1)} %pmax.7, bf16[1,1024,256]{2,1,0:T(8,128)(2,1)} %param.5, bf16[1,256,1024]{2,1,0:T(8,128)(2,1)S(1)} %all-gather, bf16[1,1024,1024]{2,1,0:T(8,128)(2,1)S(1)} %copy-done), kind=kOutput, calls=%fused_computation.12 | convolution fusion | flops 538181376 | bytes 4197376 | tf_op jit(solution)/shard_map/dot_general | solution.py:14
  84.4 19.4 %psum.15 = f32[256]{0:T(256)S(1)} all-reduce(f32[256]{0:T(256)S(1)} %get-tuple-element.4), channel_id=1, replica_groups=mesh['seq'=8,'batch'=4] {'seq'}, use_global_device_ids=true, to_apply=%region_5.0 | all-reduce | flops 256 | bytes 2048 | tf_op jit(solution)/shard_map/psum | solution.py:21
  103.7 0.0 copy-done.1
  103.7 3.0 %fusion.5 = f32[1024,256]{0,1:T(8,128)} fusion(bf16[1,1024,1024]{2,1,0:T(8,128)(2,1)S(1)} %copy-done, f32[1024,256]{1,0:T(8,128)} %get-tuple-element.5, f32[256]{0:T(256)S(1)} %psum.15, f32[256]{0:T(256)S(1)} %psum.14, f32[256]{0:T(256)S(1)} %pmax.7, bf16[1,1024,256]{2,1,0:T(8,128)(2,1)S(1)} %copy-done.1), kind=kOutput, calls=%fused_computation.6 | convolution fusion | flops 538443776 | bytes 4721664 | tf_op jit(solution)/shard_map/dot_general | solution.py:30
  106.8 0.0 reduce-scatter.2.cloned.1.call-update
  106.8 0.0 copy-done.3
  106.8 31.8 %all_gather.13 = bf16[1024,256]{1,0:T(8,128)(2,1)S(1)} all-gather(bf16[128,256]{1,0:T(8,128)(2,1)S(1)} %copy-done.3), channel_id=1, replica_groups=mesh['seq'=8,'batch'=4] {'seq'}, dimensions={0}, use_global_device_ids=true | all-gather | bytes 589824 | tf_op jit(solution)/shard_map/all_gather | solution.py:12
  138.7 0.7 fusion.12
  139.4 0.5 copy-done.2
  139.9 2.2 %fusion.4 = bf16[1,1024,1024]{2,1,0:T(8,128)(2,1)} fusion(f32[1024,1024]{1,0:T(8,128)S(1)} %fusion.12, bf16[1024,256]{1,0:T(8,128)(2,1)S(1)} %all_gather.13, f32[1024,256]{1,0:T(8,128)S(1)} %copy-done.2, f32[256]{0:T(256)S(1)} %psum.15, f32[256]{0:T(256)S(1)} %psum.14, f32[256]{0:T(256)S(1)} %pmax.7, bf16[1,1024,256]{2,1,0:T(8,128)(2,1)S(1)} %copy-done.1), kind=kOutput, calls=%fused_computation.5 | convolution fusion | flops 541589504 | bytes 8391680 | tf_op jit(solution)/shard_map/dot_general | solution.py:26
  142.1 27.1 %reduce-scatter.2.cloned.1.call-done = f32[128,256]{0,1:T(8,128)} async-done(((f32[1024,256]{0,1:T(8,128)}), f32[128,256]{0,1:T(8,128)}) %reduce-scatter.2.cloned.1.call-update) | async-done | bytes 131088 | tf_op jit(solution)/shard_map/reduce_scatter | solution.py:33
  169.1 7.4 %all-gather.1 = f32[512,256]{0,1:T(8,128)S(1)} all-gather(f32[128,256]{0,1:T(8,128)} %reduce-scatter.2.cloned.1.call-done), channel_id=3, replica_groups=mesh['seq'=8,'batch'=4] {'batch'}, dimensions={0}, use_global_device_ids=true | all-gather | bytes 655360 | tf_op jit(solution)/shard_map/all_gather | solution.py:34
  176.5 0.2 reshape.21
  176.7 0.3 reduce_sum.29
  177.0 0.8 copy.6
  (2 shorter events, 0.0 us)
Async XLA Ops:
  7.2 74.4 %copy-start = (bf16[1,1024,1024]{2,1,0:T(8,128)(2,1)S(1)}, bf16[1,1024,1024]{2,1,0:T(8,128)(2,1)}, u32[]{:S(2)}) copy-start(bf16[1,1024,1024]{2,1,0:T(8,128)(2,1)} %param.4) | copy-start | bytes 6291460
  7.2 162.0 %reduce-scatter.2.cloned.1.call-start = ((), (), s32[]{:S(2)}) async-start(), calls=%async_computation.1 | async-start | bytes 1179648 | tf_op jit(solution)/shard_map/reduce_scatter | solution.py:33
  81.5 22.2 %copy-start.1 = (bf16[1,1024,256]{2,1,0:T(8,128)(2,1)S(1)}, bf16[1,1024,256]{2,1,0:T(8,128)(2,1)}, u32[]{:S(2)}) copy-start(bf16[1,1024,256]{2,1,0:T(8,128)(2,1)} %param.5) | copy-start | bytes 1572868
  103.7 3.1 %copy-start.3 = (bf16[128,256]{1,0:T(8,128)(2,1)S(1)}, bf16[128,256]{1,0:T(8,128)(2,1)}, u32[]{:S(2)}) copy-start(bf16[128,256]{1,0:T(8,128)(2,1)} %param.7) | copy-start | bytes 196612
  138.7 1.2 copy-start.2
Sparse Core Ops, SparseCore 0:
  106.9 62.1 reduce-scatter.1
